TPU v7x, 512 devices: a whole 4x8x8 slice. The times are simulated.
512 devices in a mesh: row: 32 (over z, x), col: 16 (over y, core).
Axes of the slice: x: 4, y: 8, z: 8, core: 2. Of those that a mesh axis runs over, the one named last changes fastest.
Arguments:
- tile_values: bfloat16 [768, 2048, 128], P('row', 'col'), may hold values from -0.02734375 to 0.02734375
- tile_counts: int32 [384, 16], P('row', 'col'), may hold values from 0 to 2, as said below
- tile_cols: int32 [768, 16], P('row', 'col'), may hold values from 0 to 1, as said below
- panels: bfloat16 [49152, 4096], P('row', 'col'), may hold values from -6 to 6
Outputs:
- product: bfloat16 [4096, 4096], P('col', 'row')
Inputs may be any that keep to these rules, and one draw needn't show every extreme that they name: `tile_counts`: within each device the filled slots follow block row order; a device holds at most 24 tiles and some device holds exactly 24 in every draw. `tile_cols`: within one block row of a device the filled slots' columns rise strictly; entries of unfilled slots carry no meaning.
All inputs are finite; a program needn't handle non-finite values.
Results may differ from a plain program's by a relative error of at most 0.001.
Values may be sent and summed in bfloat16 or wider, within the bound.
A program may use at most 64 MiB of HBM per device.

v0:
```python
import jax
import jax.numpy as jnp
from jax import lax
from jax.sharding import Mesh
from jax.sharding import PartitionSpec as P

BC_DEV = 2
ROW = ("row_0", "row_1")


def scatter_axes(x, axes, dim):
    if not axes:
        return x
    nearer = lax.psum_scatter(x, axes[0], scatter_dimension=dim, tiled=True)
    return scatter_axes(nearer, axes[1:], dim)


def selection(tile_counts, tile_cols, slots, blocks_wide):
    counts = tile_counts[:, 0]
    row_start = jnp.cumsum(counts) - counts
    slot_ids = jnp.arange(slots, dtype=jnp.int32)[:, None]
    row_mask = (slot_ids >= row_start[None, :]) & (slot_ids < (row_start + counts)[None, :])
    col_mask = tile_cols == jnp.arange(blocks_wide, dtype=jnp.int32)[None, :]
    return (counts, row_mask, col_mask)


def dense_product(dense_block, b_columns):
    return lax.dot_general(
        dense_block, b_columns, (((0,), (0,)), ((), ())), preferred_element_type=jnp.float32
    )


def dense_builder(tile_values, tile_counts, tile_cols):
    slots = tile_values.shape[0]
    edge = tile_values.shape[1]
    blocks_tall = tile_counts.shape[0]
    counts, row_mask, col_mask = selection(tile_counts, tile_cols, slots, BC_DEV)
    selector = (row_mask[:, :, None] & col_mask[:, None, :]).astype(jnp.bfloat16)
    dense_block = jnp.einsum(
        "sij,sab->iajb", selector, tile_values, preferred_element_type=jnp.float32
    )
    dense_block = dense_block.astype(jnp.bfloat16).reshape(blocks_tall * edge, BC_DEV * edge)

    def tile_term(b_columns, flipped):
        return dense_product(dense_block, b_columns)

    return tile_term


def per_device(tile_values, tile_counts, tile_cols, panels):
    tile_term = dense_builder(tile_values, tile_counts, tile_cols)
    partial_value = tile_term(lax.all_gather(panels, "col", axis=1, tiled=True), False)
    result = scatter_axes(partial_value, ROW, 1)
    return result.astype(jnp.bfloat16)


def solution(mesh):
    finer = Mesh(mesh.devices.reshape(8, 4, mesh.shape["col"]), ("row_0", "row_1", "col"))
    in_specs = (P(ROW, "col", None), P(ROW, "col"), P(ROW, "col"), P(ROW, "col"))
    out_specs = P("col", ROW)
    return jax.shard_map(
        per_device, mesh=finer, in_specs=in_specs, out_specs=out_specs, check_vma=False
    )
```

profile of v0, /device:TPU:24, one launch (start us, length us, event | category | flops | bytes accessed | tf_op | source)
XLA Modules:
  0.0 200.8 jit_solution(15301291756351218175)
XLA Ops:
  6.5 0.0 all-gather.2.cloned.1.call-start
  6.5 0.7 all-gather.2.cloned.1.call-update
  7.3 0.0 reduce-scatter.3.cloned.1.call-start
  7.3 0.8 reduce-window.7
  8.1 0.7 iota_compare_fusion.2
  8.8 0.7 bitcast_subtract_fusion
  9.5 0.1 fusion.8
  9.5 1.8 fusion
  11.4 0.8 copy.7
  12.2 84.5 %all-gather.2.cloned.1.call-done = bf16[1536,4096]{1,0:T(8,128)(2,1)} async-done(((bf16[1536,256]{1,0:T(8,128)(2,1)}), bf16[1536,4096]{1,0:T(8,128)(2,1)}) %all-gather.2.cloned.1.call-update) | async-done | bytes 12582928 | tf_op jit(solution)/shard_map/all_gather | solution.py:52
  96.7 9.6 %fusion.1 = f32[256,4096]{1,0:T(8,128)} fusion(bf16[1536,4096]{1,0:T(8,128)(2,1)} %all-gather.2.cloned.1.call-done, bf16[192,8,2,128]{3,2,1,0:T(2,128)(2,1)S(1)} %bitcast.21), kind=kOutput, calls=%fused_computation.2 | convolution fusion | flops 3221225472 | bytes 17563648 | tf_op jit(solution)/shard_map/dot_general | solution.py:28
  106.2 0.0 reduce-scatter.3.cloned.1.call-update
  106.3 0.0 reduce-scatter.5.cloned.1.call-start
  106.3 58.5 %reduce-scatter.3.cloned.1.call-done = f32[256,512]{1,0:T(8,128)} async-done(((f32[256,4096]{1,0:T(8,128)}), f32[256,512]{1,0:T(8,128)}) %reduce-scatter.3.cloned.1.call-update) | async-done | bytes 524304 | tf_op jit(solution)/shard_map/reduce_scatter | solution.py:14
  164.8 0.0 reduce-scatter.5.cloned.1.call-update
  164.8 27.9 %reduce-scatter.5.cloned.1.call-done = f32[256,128]{1,0:T(8,128)} async-done(((f32[256,512]{1,0:T(8,128)}), f32[256,128]{1,0:T(8,128)}) %reduce-scatter.5.cloned.1.call-update) | async-done | bytes 131088 | tf_op jit(solution)/shard_map/reduce_scatter | solution.py:14
  192.7 1.5 convert_element_type.12
Async XLA Ops:
  6.5 90.1 %all-gather.2.cloned.1.call-start = ((), (), s32[]{:S(2)}) async-start(), calls=%async_computation.2 | async-start | bytes 13369344 | tf_op jit(solution)/shard_map/all_gather | solution.py:52
  7.3 157.5 %reduce-scatter.3.cloned.1.call-start = ((), (), s32[]{:S(2)}) async-start(), calls=%async_computation.3 | async-start | bytes 4718592 | tf_op jit(solution)/shard_map/reduce_scatter | solution.py:14
  106.3 86.4 %reduce-scatter.5.cloned.1.call-start = ((), (), s32[]{:S(2)}) async-start(), calls=%async_computation.4 | async-start | bytes 655360 | tf_op jit(solution)/shard_map/reduce_scatter | solution.py:14
Sparse Core Ops, SparseCore 0:
  9.4 87.2 all-gather.1
  106.4 58.3 reduce-scatter.2
  167.6 25.0 reduce-scatter.4
where the time goes:
time: 201 us
  waiting for transfers between devices  172 us (86%)
  between operations  13.1 us (7%)
  matrix products  11.4 us (6%)
  other arithmetic  3.77 us (2%)
    reduce_scatter x2, waiting for transfers between devices, scatter_axes(): nearer = lax.psum_scatter(x, axes[0], scatter_dimension=dim, tiled=True)  86.4 us
    all_gather x1, waiting for transfers between devices, per_device(): lax.all_gather(panels, 'col', axis=1, tiled=True)  84.5 us
    dot_general x1, matrix products, dense_product(): lax.dot_general(dense_block, b_columns, (((0,), (0,)), ((), ())), preferr...  9.58 us
  transfers between devices with their start and end apart: 3, of which 3 were waited for; matrix products, arithmetic and copies ran while one was open for 2% of the time, Pallas kernels for 0%

commit v1 on v0

v1 whole, which is shorter than its diff:
```python
import jax
import jax.numpy as jnp
from jax import lax
from jax.experimental import pallas as pl
from jax.experimental.pallas import tpu as pltpu
from jax.sharding import PartitionSpec as P

MESH = pl.DeviceIdType.MESH
NX, NZ, NY = 4, 8, 8
TILE = 128
STEPS = NY
PIECE = TILE // NZ


def kernel(
    counts, cols, tv_hbm, p_hbm, out_ref,
    tvb, a_own, a_in, bb, give1, keep, x1, give2, x2, zs, zr, cv, obuf,
    load_sem, a_send, a_recv, b_send, b_recv,
    x1_send, x1_recv, x2_send, x2_recv, z_send, z_recv, c_send, c_recv,
):
    row, col = lax.axis_index("row"), lax.axis_index("col")
    z, x = row // NX, lax.rem(row, NX)
    y, k = col // 2, lax.rem(col, 2)

    def dev(z_, x_, y_, k_):
        return (z_ * NX + x_, y_ * 2 + k_)

    right = dev(z, x, lax.rem(y + 1, NY), k)
    left = dev(z, x, lax.rem(y + NY - 1, NY), k)
    sibling = dev(z, x, y, 1 - k)
    flip = x + 1 - 2 * lax.rem(x, 2)
    bit1 = x // 2
    bit0 = lax.rem(bit1 + x, 2)
    swap = k * (NX - 1 - x - flip)
    first_x, second_x = flip + swap, NX - 1 - x - swap
    turn_bit = k * (bit1 - bit0)
    s1, s0 = bit0 + turn_bit, bit1 - turn_bit
    mate1 = dev(z, first_x, y, k)
    mate2 = dev(z, second_x, y, k)

    load_tiles = pltpu.make_async_copy(tv_hbm, tvb, load_sem.at[2])
    load_tiles.start()
    own = []
    for half in range(2):
        copy = pltpu.make_async_copy(
            p_hbm.at[:, pl.ds(half * TILE, TILE)], bb.at[0, 1 - half], load_sem.at[half]
        )
        copy.start()
        own.append(copy)

    barrier = pltpu.get_barrier_semaphore()
    peers = [right, left, sibling, mate1, mate2]
    peers += [dev(lax.rem(z + d, NZ), x, y, k) for d in range(1, NZ)]
    for peer in peers:
        pl.semaphore_signal(barrier, inc=1, device_id=peer, device_id_type=MESH)
    pl.semaphore_wait(barrier, len(peers))

    def ring_copy(src, i, c):
        return pltpu.make_async_remote_copy(
            src_ref=src,
            dst_ref=bb.at[i + 1, c],
            send_sem=b_send.at[i, c],
            recv_sem=b_recv.at[i + 1, c],
            device_id=right if c == 0 else left,
            device_id_type=MESH,
        )

    for i in range(min(2, STEPS - 1)):
        for c in range(2):
            half = (i + c) % 2
            ring_copy(p_hbm.at[:, pl.ds(half * TILE, TILE)], i, c).start()

    load_tiles.wait()

    def build(i, start):
        n = counts[i, 0]
        for b in range(2):
            slot = jnp.minimum(start + jnp.where(n == 2, b, 0), cols.shape[0] - 1)
            valid = jnp.logical_or(n == 2, jnp.logical_and(n == 1, cols[slot, 0] == b))
            tile = tvb[slot].T
            a_own[b * TILE:(b + 1) * TILE, pl.ds(pl.multiple_of(i * TILE, TILE), TILE)] = (
                jnp.where(valid, tile, jnp.zeros_like(tile))
            )
        return start + n

    lax.fori_loop(0, counts.shape[0], build, jnp.int32(0))
    a_copy = pltpu.make_async_remote_copy(
        src_ref=a_own, dst_ref=a_in, send_sem=a_send, recv_sem=a_recv,
        device_id=sibling, device_id_type=MESH,
    )
    a_copy.start()
    own[0].wait()
    own[1].wait()
    a_copy.wait()

    def x1_copy(t):
        return pltpu.make_async_remote_copy(
            src_ref=give1.at[t], dst_ref=x1.at[t],
            send_sem=x1_send.at[t], recv_sem=x1_recv.at[t], device_id=mate1, device_id_type=MESH,
        )

    def x2_copy(t):
        return pltpu.make_async_remote_copy(
            src_ref=give2.at[t], dst_ref=x2.at[t],
            send_sem=x2_send.at[t], recv_sem=x2_recv.at[t], device_id=mate2, device_id_type=MESH,
        )

    def owner_row(c, t):
        far = (t + 1) // 2
        j = lax.rem(y + NY + (far if c else -far), NY)
        half = lax.rem(t + 1 + c, 2)
        return j, 2 * k + half

    def take_block(t):
        for c in range(2):
            ring_copy(bb.at[t, c], t - 1, c).wait_recv()

            @pl.when(t < STEPS - 2)
            def _():
                ring_copy(bb.at[t, c], t + 1, c).start()

    def step(it, carry):
        @pl.when(jnp.logical_and(it >= 1, it < STEPS))
        def _():
            take_block(it)

        @pl.when(it < STEPS)
        def _():
            t = it
            for turn in range(2):
                half = (1 - s1) if turn == 0 else s1
                both = jnp.concatenate([bb[t, 0], bb[t, 1]], axis=1)
                lhs = jnp.where(half == k, a_own[...], a_in[...])
                value = jnp.dot(lhs, both, preferred_element_type=jnp.float32)
                target = give1 if turn == 0 else keep
                target[t] = value.reshape(2, NZ, PIECE, 256)
                if turn == 0:
                    x1_copy(t).start()

        @pl.when(jnp.logical_and(it >= 1, it < STEPS + 1))
        def _():
            t = it - 1
            x1_copy(t).wait_recv()
            low, high = keep[t, 0] + x1[t, 0], keep[t, 1] + x1[t, 1]
            give2[t] = jnp.where(s0 == 0, high, low)
            x2_copy(t).start()
            zs[t] = jnp.where(s0 == 0, low, high)

        @pl.when(jnp.logical_and(it >= 2, it < STEPS + 2))
        def _():
            t = it - 2
            x2_copy(t).wait_recv()
            zs[t] = zs[t] + x2[t]
            for d in sorted(range(1, NZ), key=lambda d: abs(d - NZ // 2)):
                peer = lax.rem(z + d, NZ)
                pltpu.make_async_remote_copy(
                    src_ref=zs.at[t, peer],
                    dst_ref=zr.at[t, d - 1],
                    send_sem=z_send.at[t], recv_sem=z_recv.at[t],
                    device_id=dev(peer, x, y, k), device_id_type=MESH,
                ).start()

        @pl.when(it >= 3)
        def _():
            t = it - 3
            pltpu.make_async_copy(zr.at[t], zr.at[t], z_recv.at[t]).wait()
            total = zs[t, z]
            for d in range(NZ - 1):
                total = total + zr[t, d]
            for c in range(2):
                cv[t, c] = total[:, c * TILE:(c + 1) * TILE].astype(jnp.bfloat16)
            dst_core = s1
            for c in range(2):
                j, owner_x = owner_row(c, t)
                me = jnp.logical_and(
                    jnp.logical_and(j == z, owner_x == x), dst_core == k
                )
                dst = obuf.at[s0 * NZ + z]

                @pl.when(me)
                def _():
                    copy = pltpu.make_async_copy(cv.at[t, c], dst, load_sem.at[0])
                    copy.start()
                    copy.wait()

                @pl.when(jnp.logical_not(me))
                def _():
                    pltpu.make_async_remote_copy(
                        src_ref=cv.at[t, c], dst_ref=dst,
                        send_sem=c_send.at[t, c], recv_sem=c_recv,
                        device_id=dev(j, owner_x, y, dst_core), device_id_type=MESH,
                    ).start()
        return carry

    lax.fori_loop(0, STEPS + 3, step, 0)

    has_own = jnp.logical_and(x // 2 == k, s1 == k)

    @pl.when(has_own)
    def _():
        others = obuf.at[pl.ds(0, 2 * NZ - 1)]
        pltpu.make_async_copy(others, others, c_recv).wait()

    @pl.when(jnp.logical_not(has_own))
    def _():
        pltpu.make_async_copy(obuf, obuf, c_recv).wait()

    out_ref[...] = obuf[...].reshape(256, TILE)

    def drain(t, carry):
        x1_copy(t).wait_send()
        x2_copy(t).wait_send()
        pltpu.make_async_copy(zr.at[t], zr.at[t], z_send.at[t]).wait()
        for c in range(2):
            @pl.when(t < STEPS - 1)
            def _():
                ring_copy(bb.at[t, c], t, c).wait_send()
            j, owner_x = owner_row(c, t)
            me = jnp.logical_and(
                jnp.logical_and(j == z, owner_x == x), s1 == k
            )

            @pl.when(jnp.logical_not(me))
            def _():
                pltpu.make_async_copy(cv.at[t, c], cv.at[t, c], c_send.at[t, c]).wait()
        return carry

    lax.fori_loop(0, STEPS, drain, 0)


def per_device(tile_values, tile_counts, tile_cols, panels):
    bf16, f32 = jnp.bfloat16, jnp.float32
    dma = pltpu.SemaphoreType.DMA
    return pl.pallas_call(
        kernel,
        out_shape=jax.ShapeDtypeStruct((256, TILE), bf16),
        in_specs=[
            pl.BlockSpec(memory_space=pltpu.SMEM),
            pl.BlockSpec(memory_space=pltpu.SMEM),
            pl.BlockSpec(memory_space=pl.ANY),
            pl.BlockSpec(memory_space=pl.ANY),
        ],
        out_specs=pl.BlockSpec(memory_space=pltpu.VMEM),
        scratch_shapes=[
            pltpu.VMEM(tile_values.shape, bf16),
            pltpu.VMEM((256, panels.shape[0]), bf16),
            pltpu.VMEM((256, panels.shape[0]), bf16),
            pltpu.VMEM((STEPS, 2, panels.shape[0], TILE), bf16),
            pltpu.VMEM((STEPS, 2, NZ, PIECE, 256), f32),
            pltpu.VMEM((STEPS, 2, NZ, PIECE, 256), f32),
            pltpu.VMEM((STEPS, 2, NZ, PIECE, 256), f32),
            pltpu.VMEM((STEPS, NZ, PIECE, 256), f32),
            pltpu.VMEM((STEPS, NZ, PIECE, 256), f32),
            pltpu.VMEM((STEPS, NZ, PIECE, 256), f32),
            pltpu.VMEM((STEPS, NZ - 1, PIECE, 256), f32),
            pltpu.VMEM((STEPS, 2, PIECE, TILE), bf16),
            pltpu.VMEM((2 * NZ, PIECE, TILE), bf16),
            dma((3,)), dma, dma,
            dma((STEPS - 1, 2)), dma((STEPS, 2)),
            dma((STEPS,)), dma((STEPS,)), dma((STEPS,)), dma((STEPS,)),
            dma((STEPS,)), dma((STEPS,)), dma((STEPS, 2)), dma,
        ],
        compiler_params=pltpu.CompilerParams(
            collective_id=0, has_side_effects=True, vmem_limit_bytes=48 * 1024 * 1024
        ),
    )(tile_counts, tile_cols, tile_values, panels)


def solution(mesh):
    return jax.shard_map(
        per_device,
        mesh=mesh,
        in_specs=(P("row", "col", None), P("row", "col"), P("row", "col"), P("row", "col")),
        out_specs=P("col", "row"),
        check_vma=False,
    )
```

time: 201 us -> 98.8 us (0.49)
  the two profiles are of different devices: /device:TPU:24 before, /device:TPU:33 now
where the time goes in v1:
time: 98.8 us; the launch traced here: 98.4 us
  Pallas kernels  94.6 us (96%)
  local copies, waits for them, and re-layouts  3.74 us (4%)
    pallas_call x1, Pallas kernels, per_device(): pl.pallas_call(kernel, out_shape=jax.ShapeDtypeStruct((256, TILE), bf16),...  94.6 us
    unnamed x9, local copies, waits for them, and re-layouts  3.74 us

profile of v1, /device:TPU:33, one launch (start us, length us, event | category | flops | bytes accessed | tf_op | source)
XLA Modules:
  0.0 98.4 jit_solution(10076693548003201455)
XLA Ops:
  0.0 0.0 copy-start.2
  0.0 0.8 copy.5.counts
  0.8 0.0 copy-done.2
  0.8 0.1 copy.6.cols
  0.8 0.0 copy-start
  0.8 1.1 %copy-done = bf16[24,128,128]{2,1,0:T(8,128)(2,1)S(1)} copy-done((bf16[24,128,128]{2,1,0:T(8,128)(2,1)S(1)}, bf16[24,128,128]{2,1,0:T(8,128)(2,1)}, u32[]{:S(2)}) %copy-start) | copy-done | bytes 786456
  2.0 0.0 copy-start.1
  2.0 1.1 %copy-done.1 = bf16[1536,256]{1,0:T(8,128)(2,1)S(1)} copy-done((bf16[1536,256]{1,0:T(8,128)(2,1)S(1)}, bf16[1536,256]{1,0:T(8,128)(2,1)}, u32[]{:S(2)}) %copy-start.1) | copy-done | bytes 786456
  3.1 94.6 %shard_map.46 = bf16[256,128]{1,0:T(8,128)(2,1)S(1)} custom-call(s32[12,1]{1,0:T(8,128)S(1)} %copy.5.counts, s32[24,1]{1,0:T(8,128)S(1)} %copy.6.cols, bf16[24,128,128]{2,1,0:T(8,128)(2,1)S(1)} %copy-done, bf16[1536,256]{1,0:T(8,128)(2,1)S(1)} %copy-done.1), custom_call_target="tpu_custom_call" | custom-call | tf_op jit(solution)/shard_map/pallas_call | solution.py:234
  97.7 0.6 copy.8
Async XLA Ops:
  0.0 0.8 copy-start.2
  0.8 1.1 %copy-start = (bf16[24,128,128]{2,1,0:T(8,128)(2,1)S(1)}, bf16[24,128,128]{2,1,0:T(8,128)(2,1)}, u32[]{:S(2)}) copy-start(bf16[24,128,128]{2,1,0:T(8,128)(2,1)} %tv_hbm.1) | copy-start | bytes 2359300
  2.0 1.1 %copy-start.1 = (bf16[1536,256]{1,0:T(8,128)(2,1)S(1)}, bf16[1536,256]{1,0:T(8,128)(2,1)}, u32[]{:S(2)}) copy-start(bf16[1536,256]{1,0:T(8,128)(2,1)} %p_hbm.1) | copy-start | bytes 2359300

commit v2 on v1

--- a/solution.py
+++ b/solution.py
@@ -16,7 +16,7 @@
     counts, cols, tv_hbm, p_hbm, out_ref,
     tvb, a_own, a_in, bb, give1, keep, x1, give2, x2, zs, zr, cv, obuf,
     load_sem, a_send, a_recv, b_send, b_recv,
-    x1_send, x1_recv, x2_send, x2_recv, z_send, z_recv, c_send, c_recv,
+    x1_send, x1_recv, x2_send, x2_recv, z_send, z_recv, c_send, c_recv, known,
 ):
     row, col = lax.axis_index("row"), lax.axis_index("col")
     z, x = row // NX, lax.rem(row, NX)
@@ -49,11 +49,20 @@
         own.append(copy)
 
     barrier = pltpu.get_barrier_semaphore()
-    peers = [right, left, sibling, mate1, mate2]
-    peers += [dev(lax.rem(z + d, NZ), x, y, k) for d in range(1, NZ)]
+    above = dev(lax.rem(z + 1, NZ), x, y, k)
+    below = dev(lax.rem(z + NZ - 1, NZ), x, y, k)
+    peers = [right, left, sibling, mate1, mate2, above, below]
     for peer in peers:
         pl.semaphore_signal(barrier, inc=1, device_id=peer, device_id_type=MESH)
     pl.semaphore_wait(barrier, len(peers))
+
+    def tell(r):
+        for side, peer in ((0, above), (1, below)):
+            pl.semaphore_signal(known.at[r, side], inc=1, device_id=peer, device_id_type=MESH)
+
+    def hear(r):
+        for side in range(2):
+            pl.semaphore_wait(known.at[r, side], 1)
 
     def ring_copy(src, i, c):
         return pltpu.make_async_remote_copy(
@@ -69,34 +78,40 @@
         for c in range(2):
             half = (i + c) % 2
             ring_copy(p_hbm.at[:, pl.ds(half * TILE, TILE)], i, c).start()
+    tell(0)
 
     load_tiles.wait()
 
     def build(i, start):
-        n = counts[i, 0]
+        n = counts[0, i]
         for b in range(2):
-            slot = jnp.minimum(start + jnp.where(n == 2, b, 0), cols.shape[0] - 1)
-            valid = jnp.logical_or(n == 2, jnp.logical_and(n == 1, cols[slot, 0] == b))
+            slot = jnp.minimum(start + jnp.where(n == 2, b, 0), cols.shape[1] - 1)
+            valid = jnp.logical_or(n == 2, jnp.logical_and(n == 1, cols[0, slot] == b))
             tile = tvb[slot].T
             a_own[b * TILE:(b + 1) * TILE, pl.ds(pl.multiple_of(i * TILE, TILE), TILE)] = (
                 jnp.where(valid, tile, jnp.zeros_like(tile))
             )
         return start + n
 
-    lax.fori_loop(0, counts.shape[0], build, jnp.int32(0))
+    lax.fori_loop(0, counts.shape[1], build, jnp.int32(0))
     a_copy = pltpu.make_async_remote_copy(
         src_ref=a_own, dst_ref=a_in, send_sem=a_send, recv_sem=a_recv,
         device_id=sibling, device_id_type=MESH,
     )
     a_copy.start()
+    hear(0)
+    tell(1)
     own[0].wait()
     own[1].wait()
     a_copy.wait()
-
-    def x1_copy(t):
+    hear(1)
+    tell(2)
+
+    def x1_copy(t, piece):
         return pltpu.make_async_remote_copy(
-            src_ref=give1.at[t], dst_ref=x1.at[t],
-            send_sem=x1_send.at[t], recv_sem=x1_recv.at[t], device_id=mate1, device_id_type=MESH,
+            src_ref=give1.at[t, piece], dst_ref=x1.at[t, piece],
+            send_sem=x1_send.at[t, piece], recv_sem=x1_recv.at[t, piece],
+            device_id=mate1, device_id_type=MESH,
         )
 
     def x2_copy(t):
@@ -127,30 +142,27 @@
         @pl.when(it < STEPS)
         def _():
             t = it
-            for turn in range(2):
-                half = (1 - s1) if turn == 0 else s1
-                both = jnp.concatenate([bb[t, 0], bb[t, 1]], axis=1)
-                lhs = jnp.where(half == k, a_own[...], a_in[...])
-                value = jnp.dot(lhs, both, preferred_element_type=jnp.float32)
-                target = give1 if turn == 0 else keep
-                target[t] = value.reshape(2, NZ, PIECE, 256)
-                if turn == 0:
-                    x1_copy(t).start()
+            both = jnp.concatenate([bb[t, 0], bb[t, 1]], axis=1)
+            for half, target in ((1 - s1, give1), (s1, keep)):
+                for piece in range(2):
+                    sub = (1 - s0) if piece == 0 else s0
+                    rows = pl.ds(pl.multiple_of(sub * TILE, TILE), TILE)
+                    lhs = jnp.where(half == k, a_own[rows], a_in[rows])
+                    value = jnp.dot(lhs, both, preferred_element_type=jnp.float32)
+                    target[t, piece] = value.reshape(NZ, PIECE, 256)
+                    if target is give1:
+                        x1_copy(t, piece).start()
+
+        @pl.when(it == 0)
+        def _():
+            hear(2)
 
         @pl.when(jnp.logical_and(it >= 1, it < STEPS + 1))
         def _():
             t = it - 1
-            x1_copy(t).wait_recv()
-            low, high = keep[t, 0] + x1[t, 0], keep[t, 1] + x1[t, 1]
-            give2[t] = jnp.where(s0 == 0, high, low)
-            x2_copy(t).start()
-            zs[t] = jnp.where(s0 == 0, low, high)
-
-        @pl.when(jnp.logical_and(it >= 2, it < STEPS + 2))
-        def _():
-            t = it - 2
+            x1_copy(t, 1).wait_recv()
             x2_copy(t).wait_recv()
-            zs[t] = zs[t] + x2[t]
+            zs[t] = keep[t, 1] + x1[t, 1] + x2[t]
             for d in sorted(range(1, NZ), key=lambda d: abs(d - NZ // 2)):
                 peer = lax.rem(z + d, NZ)
                 pltpu.make_async_remote_copy(
@@ -160,9 +172,9 @@
                     device_id=dev(peer, x, y, k), device_id_type=MESH,
                 ).start()
 
-        @pl.when(it >= 3)
-        def _():
-            t = it - 3
+        @pl.when(it >= 2)
+        def _():
+            t = it - 2
             pltpu.make_async_copy(zr.at[t], zr.at[t], z_recv.at[t]).wait()
             total = zs[t, z]
             for d in range(NZ - 1):
@@ -190,9 +202,16 @@
                         send_sem=c_send.at[t, c], recv_sem=c_recv,
                         device_id=dev(j, owner_x, y, dst_core), device_id_type=MESH,
                     ).start()
+        @pl.when(it < STEPS)
+        def _():
+            t = it
+            x1_copy(t, 0).wait_recv()
+            give2[t] = keep[t, 0] + x1[t, 0]
+            x2_copy(t).start()
+
         return carry
 
-    lax.fori_loop(0, STEPS + 3, step, 0)
+    lax.fori_loop(0, STEPS + 2, step, 0)
 
     has_own = jnp.logical_and(x // 2 == k, s1 == k)
 
@@ -208,7 +227,8 @@
     out_ref[...] = obuf[...].reshape(256, TILE)
 
     def drain(t, carry):
-        x1_copy(t).wait_send()
+        x1_copy(t, 0).wait_send()
+        x1_copy(t, 1).wait_send()
         x2_copy(t).wait_send()
         pltpu.make_async_copy(zr.at[t], zr.at[t], z_send.at[t]).wait()
         for c in range(2):
@@ -257,13 +277,14 @@
             pltpu.VMEM((2 * NZ, PIECE, TILE), bf16),
             dma((3,)), dma, dma,
             dma((STEPS - 1, 2)), dma((STEPS, 2)),
-            dma((STEPS,)), dma((STEPS,)), dma((STEPS,)), dma((STEPS,)),
+            dma((STEPS, 2)), dma((STEPS, 2)), dma((STEPS,)), dma((STEPS,)),
             dma((STEPS,)), dma((STEPS,)), dma((STEPS, 2)), dma,
+            pltpu.SemaphoreType.REGULAR((3, 2)),
         ],
         compiler_params=pltpu.CompilerParams(
-            collective_id=0, has_side_effects=True, vmem_limit_bytes=48 * 1024 * 1024
+            collective_id=0, has_side_effects=True, vmem_limit_bytes=60 * 1024 * 1024
         ),
-    )(tile_counts, tile_cols, tile_values, panels)
+    )(tile_counts.T, tile_cols.T, tile_values, panels)
 
 
 def solution(mesh):

time: 98.8 us -> 94.6 us (0.957)
  local copies, waits for them, and re-layouts: 3.74 us -> 1.47 us
  Pallas kernels: 94.6 us -> 92.7 us
    unnamed x9 -> x1, local copies, waits for them, and re-layouts: 3.74 us -> 1.47 us
    pallas_call x1, Pallas kernels: 94.6 us -> 92.7 us  [per_device(): pl.pallas_call(kernel, out_shape=jax.ShapeDtypeStruct((256, TILE), bf16),...]
where the time goes in v2:
time: 94.6 us; the launch traced here: 94.2 us
  Pallas kernels  92.7 us (98%)
  local copies, waits for them, and re-layouts  1.47 us (2%)
    pallas_call x1, Pallas kernels, per_device(): pl.pallas_call(kernel, out_shape=jax.ShapeDtypeStruct((256, TILE), bf16),...  92.7 us

profile of v2, /device:TPU:33, one launch (start us, length us, event | category | flops | bytes accessed | tf_op | source)
XLA Modules:
  0.0 94.2 jit_solution(5277090211938655230)
XLA Ops:
  0.0 92.7 %shard_map.46 = bf16[256,128]{1,0:T(8,128)(2,1)} custom-call(s32[1,12]{1,0:T(1,128)} %bitcast.2, s32[1,24]{1,0:T(1,128)} %bitcast.3, bf16[24,128,128]{2,1,0:T(8,128)(2,1)} %tv_hbm.1, bf16[1536,256]{1,0:T(8,128)(2,1)} %p_hbm.1), custom_call_target="tpu_custom_call" | custom-call | tf_op jit(solution)/shard_map/pallas_call | solution.py:254
  92.7 1.5 %copy.6 = bf16[256,128]{1,0:T(8,128)(2,1)} copy(bf16[256,128]{1,0:T(8,128)(2,1)} %shard_map.46) | data formatting | bytes 131072

commit v3 on v0

v3 whole, which is shorter than its diff:
```python
import jax
import jax.numpy as jnp
from jax import lax
from jax.experimental import pallas as pl
from jax.experimental.pallas import tpu as pltpu
from jax.sharding import PartitionSpec as P

MESH = pl.DeviceIdType.MESH
NX, NZ, NY = 4, 8, 8
TILE = 128
STEPS = NY
LAST = STEPS - 1
PIECE = 2 * TILE // NZ


def kernel(
    counts, cols, tv_hbm, p_hbm, out_ref,
    tvb, a_own, a_in, a_mate, bb, give, keep, x2, zs, zr, cv, obuf,
    load_sem, a_send, a_recv, b_send, b_recv, e_send, e_recv, m_send, m_recv,
    x2_send, x2_recv, z_send, z_recv, c_send, c_recv, known,
):
    row, col = lax.axis_index("row"), lax.axis_index("col")
    z, x = row // NX, lax.rem(row, NX)
    y, k = col // 2, lax.rem(col, 2)
    depth = p_hbm.shape[0]
    half_depth = depth // 2

    def dev(z_, x_, y_, k_):
        return (z_ * NX + x_, y_ * 2 + k_)

    right = dev(z, x, lax.rem(y + 1, NY), k)
    left = dev(z, x, lax.rem(y + NY - 1, NY), k)
    above = dev(lax.rem(z + 1, NZ), x, y, k)
    below = dev(lax.rem(z + NZ - 1, NZ), x, y, k)
    sibling = dev(z, x, y, 1 - k)
    flip = x + 1 - 2 * lax.rem(x, 2)
    bit1 = x // 2
    bit0 = lax.rem(bit1 + x, 2)
    swap = k * (NX - 1 - x - flip)
    turn_bit = k * (bit1 - bit0)
    s1, s0 = bit0 + turn_bit, bit1 - turn_bit
    mate1 = dev(z, flip + swap, y, k)
    mate2 = dev(z, NX - 1 - x - swap, y, k)
    owner_x = 2 * k + s1

    def remote(src, dst, send, recv, to):
        return pltpu.make_async_remote_copy(
            src_ref=src, dst_ref=dst, send_sem=send, recv_sem=recv,
            device_id=to, device_id_type=MESH,
        )

    load_tiles = pltpu.make_async_copy(tv_hbm, tvb, load_sem.at[0])
    load_tiles.start()
    own_columns = p_hbm.at[:, pl.ds(pl.multiple_of(s1 * TILE, TILE), TILE)]
    mate_columns = p_hbm.at[:, pl.ds(pl.multiple_of((1 - s1) * TILE, TILE), TILE)]
    load_own = pltpu.make_async_copy(own_columns, bb.at[0, 0], load_sem.at[1])
    load_own.start()

    barrier = pltpu.get_barrier_semaphore()
    peers = [right, left, sibling, mate1, mate2, above, below]
    for peer in peers:
        pl.semaphore_signal(barrier, inc=1, device_id=peer, device_id_type=MESH)
    pl.semaphore_wait(barrier, len(peers))

    def tell(r):
        for side, peer in ((0, above), (1, below)):
            pl.semaphore_signal(known.at[r, side], inc=1, device_id=peer, device_id_type=MESH)

    def hear(r):
        for side in range(2):
            pl.semaphore_wait(known.at[r, side], 1)

    def ring_copy(src, i, c):
        return remote(src, bb.at[i + 1, c], b_send.at[i, c], b_recv.at[i + 1, c], left if c else right)

    def end_copy(part, c):
        rows = pl.ds(c * half_depth, half_depth)
        src = bb.at[LAST - 2 + part, c, rows]
        return remote(src, bb.at[LAST, part, rows], e_send.at[part, c], e_recv.at[part, c], left if c else right)

    first = [ring_copy(own_columns, 0, c) for c in range(2)]
    for copy in first:
        copy.start()
    merge = remote(mate_columns, bb.at[0, 1], m_send.at[2], m_recv.at[2], mate1)
    merge.start()
    tell(0)

    load_tiles.wait()

    def build(i, start):
        n = counts[0, i]
        for b in range(2):
            slot = jnp.minimum(start + jnp.where(n == 2, b, 0), cols.shape[1] - 1)
            valid = jnp.logical_or(n == 2, jnp.logical_and(n == 1, cols[0, slot] == b))
            tile = tvb[slot].T
            a_own[b * TILE:(b + 1) * TILE, pl.ds(pl.multiple_of(i * TILE, TILE), TILE)] = (
                jnp.where(valid, tile, jnp.zeros_like(tile))
            )
        return start + n

    lax.fori_loop(0, counts.shape[1], build, jnp.int32(0))
    a_copy = remote(a_own, a_in, a_send, a_recv, sibling)
    a_copy.start()
    mate_own = remote(a_own, a_mate.at[0], m_send.at[0], m_recv.at[0], mate1)
    mate_own.start()
    hear(0)
    tell(1)
    a_copy.wait()
    mate_in = remote(a_in, a_mate.at[1], m_send.at[1], m_recv.at[1], mate1)
    mate_in.start()
    hear(1)
    tell(2)

    merge.wait_recv()
    second = [ring_copy(bb.at[0, 1], 1, c) for c in range(2)]
    for copy in second:
        copy.start()

    sent = first + second + [mate_own, mate_in, merge]

    def take(t):
        for c in range(2):
            if t == LAST:
                for part in range(2):
                    end_copy(part, c).wait_recv()
                continue
            ring_copy(bb.at[0, 0], t - 1, c).wait_recv()
            if t <= LAST - 3:
                copy = ring_copy(bb.at[t, c], t + 1, c)
            else:
                copy = end_copy(t - (LAST - 2), c)
            copy.start()
            sent.append(copy)

    def blocks(s):
        if s == 0:
            return bb[0, 0], bb[0, 1]
        if s == LAST:
            return bb[LAST, 0], bb[LAST, 1]
        if s % 2:
            return bb[s, 0], bb[s + 1, 0]
        return bb[s - 1, 1], bb[s, 1]

    def x2_copy(s):
        return remote(give.at[s], x2.at[s], x2_send.at[s], x2_recv.at[s], mate2)

    def multiply(s):
        mine, mates = blocks(s)
        for core, target in ((1 - s0, give), (s0, keep)):
            lhs = jnp.where(core == k, a_own[...], a_in[...])
            value = jnp.dot(lhs, mine, preferred_element_type=jnp.float32)
            lhs = jnp.where(core == k, a_mate[0], a_mate[1])
            value += jnp.dot(lhs, mates, preferred_element_type=jnp.float32)
            target[s] = value.reshape(NZ, PIECE, TILE)
            if target is give:
                copy = x2_copy(s)
                copy.start()
                sent.append(copy)

    def spread(s):
        x2_copy(s).wait_recv()
        zs[s] = keep[s] + x2[s]
        for d in sorted(range(1, NZ), key=lambda d: abs(d - NZ // 2)):
            peer = lax.rem(z + d, NZ)
            remote(
                zs.at[s, peer], zr.at[s, d - 1], z_send.at[s], z_recv.at[s], dev(peer, x, y, k)
            ).start()

    def owner(s):
        j = lax.rem(y + NY + (-((s + 1) // 2) if s % 2 else s // 2), NY)
        me = jnp.logical_and(j == z, jnp.logical_and(owner_x == x, s0 == k))
        return j, me

    def deliver(s):
        pltpu.make_async_copy(zr.at[s], zr.at[s], z_recv.at[s]).wait()
        total = zs[s, z]
        for d in range(NZ - 1):
            total = total + zr[s, d]
        cv[s] = total.astype(jnp.bfloat16)
        j, me = owner(s)

        @pl.when(me)
        def _():
            copy = pltpu.make_async_copy(cv.at[s], obuf.at[z], load_sem.at[0])
            copy.start()
            copy.wait()

        @pl.when(jnp.logical_not(me))
        def _():
            remote(cv.at[s], obuf.at[z], c_send.at[s], c_recv, dev(j, owner_x, y, s0)).start()

    load_own.wait()
    take(1)
    if LAST > 2:
        take(2)
    hear(2)
    mate_own.wait_recv()
    mate_in.wait_recv()
    for s in range(STEPS + 2):
        if s == LAST:
            take(LAST)
        elif 2 <= s < LAST - 1:
            take(s + 1)
        if s < STEPS:
            multiply(s)
        if 1 <= s < STEPS + 1:
            spread(s - 1)
        if s >= 2:
            deliver(s - 2)

    has_own = jnp.logical_and(owner_x == x, s0 == k)

    @pl.when(has_own)
    def _():
        others = obuf.at[pl.ds(0, NZ - 1)]
        pltpu.make_async_copy(others, others, c_recv).wait()

    @pl.when(jnp.logical_not(has_own))
    def _():
        pltpu.make_async_copy(obuf, obuf, c_recv).wait()

    out_ref[...] = obuf[...].reshape(2 * TILE, TILE)

    for copy in sent:
        copy.wait_send()
    for s in range(STEPS):
        pltpu.make_async_copy(zr.at[s], zr.at[s], z_send.at[s]).wait()
        _, me = owner(s)

        @pl.when(jnp.logical_not(me))
        def _():
            pltpu.make_async_copy(cv.at[s], cv.at[s], c_send.at[s]).wait()


def per_device(tile_values, tile_counts, tile_cols, panels):
    bf16, f32 = jnp.bfloat16, jnp.float32
    dma = pltpu.SemaphoreType.DMA
    depth = panels.shape[0]
    return pl.pallas_call(
        kernel,
        out_shape=jax.ShapeDtypeStruct((2 * TILE, TILE), bf16),
        in_specs=[
            pl.BlockSpec(memory_space=pltpu.SMEM),
            pl.BlockSpec(memory_space=pltpu.SMEM),
            pl.BlockSpec(memory_space=pl.ANY),
            pl.BlockSpec(memory_space=pl.ANY),
        ],
        out_specs=pl.BlockSpec(memory_space=pltpu.VMEM),
        scratch_shapes=[
            pltpu.VMEM(tile_values.shape, bf16),
            pltpu.VMEM((2 * TILE, depth), bf16),
            pltpu.VMEM((2 * TILE, depth), bf16),
            pltpu.VMEM((2, 2 * TILE, depth), bf16),
            pltpu.VMEM((STEPS, 2, depth, TILE), bf16),
            pltpu.VMEM((STEPS, NZ, PIECE, TILE), f32),
            pltpu.VMEM((STEPS, NZ, PIECE, TILE), f32),
            pltpu.VMEM((STEPS, NZ, PIECE, TILE), f32),
            pltpu.VMEM((STEPS, NZ, PIECE, TILE), f32),
            pltpu.VMEM((STEPS, NZ - 1, PIECE, TILE), f32),
            pltpu.VMEM((STEPS, PIECE, TILE), bf16),
            pltpu.VMEM((NZ, PIECE, TILE), bf16),
            dma((2,)), dma, dma,
            dma((STEPS, 2)), dma((STEPS, 2)), dma((2, 2)), dma((2, 2)), dma((3,)), dma((3,)),
            dma((STEPS,)), dma((STEPS,)), dma((STEPS,)), dma((STEPS,)), dma((STEPS,)), dma,
            pltpu.SemaphoreType.REGULAR((3, 2)),
        ],
        compiler_params=pltpu.CompilerParams(
            collective_id=0, has_side_effects=True, vmem_limit_bytes=60 * 1024 * 1024
        ),
    )(tile_counts.T, tile_cols.T, tile_values, panels)


def solution(mesh):
    return jax.shard_map(
        per_device,
        mesh=mesh,
        in_specs=(P("row", "col", None), P("row", "col"), P("row", "col"), P("row", "col")),
        out_specs=P("col", "row"),
        check_vma=False,
    )
```

time: 201 us -> 90.6 us (0.45)
  the two profiles are of different devices: /device:TPU:24 before, /device:TPU:33 now
where the time goes in v3:
time: 90.6 us; the launch traced here: 90.4 us
  Pallas kernels  88.9 us (98%)
  local copies, waits for them, and re-layouts  1.47 us (2%)
    pallas_call x1, Pallas kernels, per_device(): pl.pallas_call(kernel, out_shape=jax.ShapeDtypeStruct((2 * TILE, TILE), b...  88.9 us

profile of v3, /device:TPU:33, one launch (start us, length us, event | category | flops | bytes accessed | tf_op | source)
XLA Modules:
  0.0 90.4 jit_solution(14685084705964585797)
XLA Ops:
  0.0 88.9 %shard_map.46 = bf16[256,128]{1,0:T(8,128)(2,1)} custom-call(s32[1,12]{1,0:T(1,128)} %bitcast.2, s32[1,24]{1,0:T(1,128)} %bitcast.3, bf16[24,128,128]{2,1,0:T(8,128)(2,1)} %tv_hbm.1, bf16[1536,256]{1,0:T(8,128)(2,1)} %p_hbm.1), custom_call_target="tpu_custom_call" | custom-call | tf_op jit(solution)/shard_map/pallas_call | solution.py:239
  88.9 1.5 %copy.6 = bf16[256,128]{1,0:T(8,128)(2,1)} copy(bf16[256,128]{1,0:T(8,128)(2,1)} %shard_map.46) | data formatting | bytes 131072

commit v4 on v3

--- a/solution.py
+++ b/solution.py
@@ -93,9 +93,12 @@
             slot = jnp.minimum(start + jnp.where(n == 2, b, 0), cols.shape[1] - 1)
             valid = jnp.logical_or(n == 2, jnp.logical_and(n == 1, cols[0, slot] == b))
             tile = tvb[slot].T
-            a_own[b * TILE:(b + 1) * TILE, pl.ds(pl.multiple_of(i * TILE, TILE), TILE)] = (
-                jnp.where(valid, tile, jnp.zeros_like(tile))
-            )
+            tile = jnp.where(valid, tile, jnp.zeros_like(tile))
+            for q in range(TILE // PIECE):
+                place = lax.rem(b * (TILE // PIECE) + q - z + 2 * NZ - 2, NZ)
+                rows = pl.ds(pl.multiple_of(place * PIECE, PIECE), PIECE)
+                lanes = pl.ds(pl.multiple_of(i * TILE, TILE), TILE)
+                a_own[rows, lanes] = tile[q * PIECE:(q + 1) * PIECE]
         return start + n
 
     lax.fori_loop(0, counts.shape[1], build, jnp.int32(0))
@@ -118,12 +121,12 @@
 
     sent = first + second + [mate_own, mate_in, merge]
 
+    def take_end(part):
+        for c in range(2):
+            end_copy(part, c).wait_recv()
+
     def take(t):
         for c in range(2):
-            if t == LAST:
-                for part in range(2):
-                    end_copy(part, c).wait_recv()
-                continue
             ring_copy(bb.at[0, 0], t - 1, c).wait_recv()
             if t <= LAST - 3:
                 copy = ring_copy(bb.at[t, c], t + 1, c)
@@ -134,37 +137,58 @@
 
     def blocks(s):
         if s == 0:
-            return bb[0, 0], bb[0, 1]
-        if s == LAST:
-            return bb[LAST, 0], bb[LAST, 1]
-        if s % 2:
-            return bb[s, 0], bb[s + 1, 0]
-        return bb[s - 1, 1], bb[s, 1]
-
-    def x2_copy(s):
-        return remote(give.at[s], x2.at[s], x2_send.at[s], x2_recv.at[s], mate2)
+            slots = (0, 0), (0, 1)
+        elif s == LAST:
+            slots = (LAST, 0), (LAST, 1)
+        elif s % 2:
+            slots = (s, 0), (s + 1, 0)
+        else:
+            slots = (s - 1, 1), (s, 1)
+        return [lambda slot=slot: bb[slot] for slot in slots]
+
+    def x2_copy(s, part):
+        places = pl.ds(part * (NZ // 2), NZ // 2)
+        return remote(
+            give.at[s, places], x2.at[s, places], x2_send.at[s, part], x2_recv.at[s, part], mate2
+        )
+
+    def product(core, rows, mates, right_side):
+        own, other = (a_mate.at[0], a_mate.at[1]) if mates else (a_own, a_in)
+        lhs = jnp.where(core == k, own[rows], other[rows])
+        return jnp.dot(lhs, right_side, preferred_element_type=jnp.float32).reshape(-1, PIECE, TILE)
+
+    GIVEN = ((slice(0, TILE), slice(0, NZ // 2)), (slice(TILE, 2 * TILE), slice(NZ // 2, NZ)))
+    KEPT = (slice(0, 2 * TILE), slice(0, NZ))
 
     def multiply(s):
         mine, mates = blocks(s)
-        for core, target in ((1 - s0, give), (s0, keep)):
-            lhs = jnp.where(core == k, a_own[...], a_in[...])
-            value = jnp.dot(lhs, mine, preferred_element_type=jnp.float32)
-            lhs = jnp.where(core == k, a_mate[0], a_mate[1])
-            value += jnp.dot(lhs, mates, preferred_element_type=jnp.float32)
-            target[s] = value.reshape(NZ, PIECE, TILE)
-            if target is give:
-                copy = x2_copy(s)
-                copy.start()
-                sent.append(copy)
+        if s == LAST:
+            take_end(0)
+            for rows, places in GIVEN:
+                give[s, places] = product(1 - s0, rows, False, bb[LAST, 0])
+            keep[s] = product(s0, KEPT[0], False, bb[LAST, 0])
+            take_end(1)
+        for part, (rows, places) in enumerate(GIVEN):
+            value = give[s, places] if s == LAST else product(1 - s0, rows, False, mine())
+            give[s, places] = value + product(1 - s0, rows, True, mates())
+            copy = x2_copy(s, part)
+            copy.start()
+            sent.append(copy)
+        value = keep[s] if s == LAST else product(s0, KEPT[0], False, mine())
+        keep[s] = value + product(s0, KEPT[0], True, mates())
 
     def spread(s):
-        x2_copy(s).wait_recv()
-        zs[s] = keep[s] + x2[s]
-        for d in sorted(range(1, NZ), key=lambda d: abs(d - NZ // 2)):
-            peer = lax.rem(z + d, NZ)
-            remote(
-                zs.at[s, peer], zr.at[s, d - 1], z_send.at[s], z_recv.at[s], dev(peer, x, y, k)
-            ).start()
+        for part, (_, places) in enumerate(GIVEN):
+            x2_copy(s, part).wait_recv()
+            zs[s, places] = keep[s, places] + x2[s, places]
+            ways = [(p, (p + 2) % NZ) for p in range(places.start, places.stop)]
+            for p, d in sorted(ways, key=lambda way: abs(way[1] - NZ // 2)):
+                if d == 0:
+                    continue
+                remote(
+                    zs.at[s, p], zr.at[s, d - 1], z_send.at[s], z_recv.at[s],
+                    dev(lax.rem(z + d, NZ), x, y, k),
+                ).start()
 
     def owner(s):
         j = lax.rem(y + NY + (-((s + 1) // 2) if s % 2 else s // 2), NY)
@@ -173,7 +197,7 @@
 
     def deliver(s):
         pltpu.make_async_copy(zr.at[s], zr.at[s], z_recv.at[s]).wait()
-        total = zs[s, z]
+        total = zs[s, NZ - 2]
         for d in range(NZ - 1):
             total = total + zr[s, d]
         cv[s] = total.astype(jnp.bfloat16)
@@ -197,9 +221,7 @@
     mate_own.wait_recv()
     mate_in.wait_recv()
     for s in range(STEPS + 2):
-        if s == LAST:
-            take(LAST)
-        elif 2 <= s < LAST - 1:
+        if 2 <= s < LAST - 1:
             take(s + 1)
         if s < STEPS:
             multiply(s)
@@ -261,11 +283,11 @@
             pltpu.VMEM((NZ, PIECE, TILE), bf16),
             dma((2,)), dma, dma,
             dma((STEPS, 2)), dma((STEPS, 2)), dma((2, 2)), dma((2, 2)), dma((3,)), dma((3,)),
-            dma((STEPS,)), dma((STEPS,)), dma((STEPS,)), dma((STEPS,)), dma((STEPS,)), dma,
+            dma((STEPS, 2)), dma((STEPS, 2)), dma((STEPS,)), dma((STEPS,)), dma((STEPS,)), dma,
             pltpu.SemaphoreType.REGULAR((3, 2)),
         ],
         compiler_params=pltpu.CompilerParams(
-            collective_id=0, has_side_effects=True, vmem_limit_bytes=60 * 1024 * 1024
+            collective_id=0, has_side_effects=True, vmem_limit_bytes=55000 * 1024
         ),
     )(tile_counts.T, tile_cols.T, tile_values, panels)
 

time: 90.6 us -> 89.2 us (0.985)
  Pallas kernels: 88.9 us -> 87.8 us
    pallas_call x1, Pallas kernels: 88.9 us -> 87.8 us  [per_device(): pl.pallas_call(kernel, out_shape=jax.ShapeDtypeStruct((2 * TILE, TILE), b...]
where the time goes in v4:
time: 89.2 us; the launch traced here: 89.1 us
  Pallas kernels  87.8 us (98%)
  local copies, waits for them, and re-layouts  1.3 us (1%)
    pallas_call x1, Pallas kernels, per_device(): pl.pallas_call(kernel, out_shape=jax.ShapeDtypeStruct((2 * TILE, TILE), b...  87.8 us

profile of v4, /device:TPU:33, one launch (start us, length us, event | category | flops | bytes accessed | tf_op | source)
XLA Modules:
  0.0 89.1 jit_solution(607112626933023867)
XLA Ops:
  0.0 0.0 copy-start
  0.0 0.0 copy-start.1
  0.0 0.7 copy-done
  0.7 0.0 copy-done.1
  0.7 87.8 %shard_map.46 = bf16[256,128]{1,0:T(8,128)(2,1)S(1)} custom-call(s32[1,12]{1,0:T(1,128)S(1)} %bitcast.2, s32[1,24]{1,0:T(1,128)S(1)} %bitcast.3, bf16[24,128,128]{2,1,0:T(8,128)(2,1)} %tv_hbm.1, bf16[1536,256]{1,0:T(8,128)(2,1)} %p_hbm.1), custom_call_target="tpu_custom_call" | custom-call | tf_op jit(solution)/shard_map/pallas_call | solution.py:261
  88.5 0.6 copy.6
Async XLA Ops:
  0.0 0.7 copy-start
  0.0 0.7 copy-start.1

commit v5 on v4

--- a/solution.py
+++ b/solution.py
@@ -14,8 +14,8 @@
 
 
 def kernel(
-    counts, cols, tv_hbm, p_hbm, out_ref,
-    tvb, a_own, a_in, a_mate, bb, give, keep, x2, zs, zr, cv, obuf,
+    counts_any, cols_any, tv_hbm, p_hbm, out_ref,
+    counts, cols, tvb, a_own, a_in, a_mate, bb, give, keep, x2, zs, zr, cv, obuf,
     load_sem, a_send, a_recv, b_send, b_recv, e_send, e_recv, m_send, m_recv,
     x2_send, x2_recv, z_send, z_recv, c_send, c_recv, known,
 ):
@@ -49,17 +49,22 @@
             device_id=to, device_id_type=MESH,
         )
 
+    barrier = pltpu.get_barrier_semaphore()
+    peers = [right, left, sibling, mate1, mate2, above, below]
+    for peer in peers:
+        pl.semaphore_signal(barrier, inc=1, device_id=peer, device_id_type=MESH)
+
     load_tiles = pltpu.make_async_copy(tv_hbm, tvb, load_sem.at[0])
     load_tiles.start()
+    load_counts = pltpu.make_async_copy(counts_any, counts, load_sem.at[2])
+    load_counts.start()
+    load_cols = pltpu.make_async_copy(cols_any, cols, load_sem.at[3])
+    load_cols.start()
     own_columns = p_hbm.at[:, pl.ds(pl.multiple_of(s1 * TILE, TILE), TILE)]
     mate_columns = p_hbm.at[:, pl.ds(pl.multiple_of((1 - s1) * TILE, TILE), TILE)]
     load_own = pltpu.make_async_copy(own_columns, bb.at[0, 0], load_sem.at[1])
     load_own.start()
 
-    barrier = pltpu.get_barrier_semaphore()
-    peers = [right, left, sibling, mate1, mate2, above, below]
-    for peer in peers:
-        pl.semaphore_signal(barrier, inc=1, device_id=peer, device_id_type=MESH)
     pl.semaphore_wait(barrier, len(peers))
 
     def tell(r):
@@ -86,6 +91,8 @@
     tell(0)
 
     load_tiles.wait()
+    load_counts.wait()
+    load_cols.wait()
 
     def build(i, start):
         n = counts[0, i]
@@ -262,13 +269,15 @@
         kernel,
         out_shape=jax.ShapeDtypeStruct((2 * TILE, TILE), bf16),
         in_specs=[
-            pl.BlockSpec(memory_space=pltpu.SMEM),
-            pl.BlockSpec(memory_space=pltpu.SMEM),
+            pl.BlockSpec(memory_space=pl.ANY),
+            pl.BlockSpec(memory_space=pl.ANY),
             pl.BlockSpec(memory_space=pl.ANY),
             pl.BlockSpec(memory_space=pl.ANY),
         ],
         out_specs=pl.BlockSpec(memory_space=pltpu.VMEM),
         scratch_shapes=[
+            pltpu.SMEM((1, tile_counts.shape[0]), jnp.int32),
+            pltpu.SMEM((1, tile_cols.shape[0]), jnp.int32),
             pltpu.VMEM(tile_values.shape, bf16),
             pltpu.VMEM((2 * TILE, depth), bf16),
             pltpu.VMEM((2 * TILE, depth), bf16),
@@ -281,7 +290,7 @@
             pltpu.VMEM((STEPS, NZ - 1, PIECE, TILE), f32),
             pltpu.VMEM((STEPS, PIECE, TILE), bf16),
             pltpu.VMEM((NZ, PIECE, TILE), bf16),
-            dma((2,)), dma, dma,
+            dma((4,)), dma, dma,
             dma((STEPS, 2)), dma((STEPS, 2)), dma((2, 2)), dma((2, 2)), dma((3,)), dma((3,)),
             dma((STEPS, 2)), dma((STEPS, 2)), dma((STEPS,)), dma((STEPS,)), dma((STEPS,)), dma,
             pltpu.SemaphoreType.REGULAR((3, 2)),

time: 89.2 us -> 88.7 us (level)
  no operation moved by 1% of the time
where the time goes in v5:
time: 88.7 us; the launch traced here: 88.6 us
  Pallas kernels  87.3 us (98%)
  local copies, waits for them, and re-layouts  1.3 us (1%)
    pallas_call x1, Pallas kernels, per_device(): pl.pallas_call(kernel, out_shape=jax.ShapeDtypeStruct((2 * TILE, TILE), b...  87.3 us

profile of v5, /device:TPU:33, one launch (start us, length us, event | category | flops | bytes accessed | tf_op | source)
XLA Modules:
  0.0 88.6 jit_solution(13717387162319491910)
XLA Ops:
  0.0 0.0 copy-start
  0.0 0.0 copy-start.1
  0.0 0.7 copy-done
  0.7 0.0 copy-done.1
  0.7 87.3 %shard_map.46 = bf16[256,128]{1,0:T(8,128)(2,1)S(1)} custom-call(s32[1,12]{1,0:T(1,128)S(1)} %bitcast.2, s32[1,24]{1,0:T(1,128)S(1)} %bitcast.3, bf16[24,128,128]{2,1,0:T(8,128)(2,1)} %tv_hbm.1, bf16[1536,256]{1,0:T(8,128)(2,1)} %p_hbm.1), custom_call_target="tpu_custom_call" | custom-call | tf_op jit(solution)/shard_map/pallas_call | solution.py:268
  88.0 0.6 copy.6
Async XLA Ops:
  0.0 0.7 copy-start
  0.0 0.7 copy-start.1

commit v6 on v5

--- a/solution.py
+++ b/solution.py
@@ -36,8 +36,8 @@
     flip = x + 1 - 2 * lax.rem(x, 2)
     bit1 = x // 2
     bit0 = lax.rem(bit1 + x, 2)
-    swap = k * (NX - 1 - x - flip)
-    turn_bit = k * (bit1 - bit0)
+    swap = (1 - k) * (NX - 1 - x - flip)
+    turn_bit = (1 - k) * (bit1 - bit0)
     s1, s0 = bit0 + turn_bit, bit1 - turn_bit
     mate1 = dev(z, flip + swap, y, k)
     mate2 = dev(z, NX - 1 - x - swap, y, k)
@@ -167,21 +167,21 @@
     GIVEN = ((slice(0, TILE), slice(0, NZ // 2)), (slice(TILE, 2 * TILE), slice(NZ // 2, NZ)))
     KEPT = (slice(0, 2 * TILE), slice(0, NZ))
 
+    def ahead(s):
+        mine, _ = blocks(s)
+        for rows, places in GIVEN:
+            give[s, places] = product(1 - s0, rows, False, mine())
+        keep[s] = product(s0, KEPT[0], False, mine())
+
     def multiply(s):
         mine, mates = blocks(s)
-        if s == LAST:
-            take_end(0)
-            for rows, places in GIVEN:
-                give[s, places] = product(1 - s0, rows, False, bb[LAST, 0])
-            keep[s] = product(s0, KEPT[0], False, bb[LAST, 0])
-            take_end(1)
         for part, (rows, places) in enumerate(GIVEN):
-            value = give[s, places] if s == LAST else product(1 - s0, rows, False, mine())
+            value = give[s, places] if s >= LAST - 2 else product(1 - s0, rows, False, mine())
             give[s, places] = value + product(1 - s0, rows, True, mates())
             copy = x2_copy(s, part)
             copy.start()
             sent.append(copy)
-        value = keep[s] if s == LAST else product(s0, KEPT[0], False, mine())
+        value = keep[s] if s >= LAST - 2 else product(s0, KEPT[0], False, mine())
         keep[s] = value + product(s0, KEPT[0], True, mates())
 
     def spread(s):
@@ -230,12 +230,20 @@
     for s in range(STEPS + 2):
         if 2 <= s < LAST - 1:
             take(s + 1)
+        if s == LAST:
+            take_end(0)
+            ahead(LAST)
+            spread(LAST - 1)
+            take_end(1)
         if s < STEPS:
             multiply(s)
-        if 1 <= s < STEPS + 1:
+        if 1 <= s < STEPS + 1 and s != LAST:
             spread(s - 1)
         if s >= 2:
             deliver(s - 2)
+        if s == LAST - 3:
+            ahead(LAST - 2)
+            ahead(LAST - 1)
 
     has_own = jnp.logical_and(owner_x == x, s0 == k)
 

time: 88.7 us -> 87.9 us (level)
  the two profiles are of different devices: /device:TPU:33 before, /device:TPU:35 now
where the time goes in v6:
time: 87.9 us; the launch traced here: 87.8 us
  Pallas kernels  86.4 us (98%)
  local copies, waits for them, and re-layouts  1.3 us (1%)
    pallas_call x1, Pallas kernels, per_device(): pl.pallas_call(kernel, out_shape=jax.ShapeDtypeStruct((2 * TILE, TILE), b...  86.4 us

profile of v6, /device:TPU:35, one launch (start us, length us, event | category | flops | bytes accessed | tf_op | source)
XLA Modules:
  0.0 87.8 jit_solution(2472993551785643733)
XLA Ops:
  0.0 0.0 copy-start
  0.0 0.0 copy-start.1
  0.0 0.7 copy-done
  0.7 0.0 copy-done.1
  0.7 86.4 %shard_map.46 = bf16[256,128]{1,0:T(8,128)(2,1)S(1)} custom-call(s32[1,12]{1,0:T(1,128)S(1)} %bitcast.2, s32[1,24]{1,0:T(1,128)S(1)} %bitcast.3, bf16[24,128,128]{2,1,0:T(8,128)(2,1)} %tv_hbm.1, bf16[1536,256]{1,0:T(8,128)(2,1)} %p_hbm.1), custom_call_target="tpu_custom_call" | custom-call | tf_op jit(solution)/shard_map/pallas_call | solution.py:276
  87.1 0.6 copy.6
Async XLA Ops:
  0.0 0.7 copy-start
  0.0 0.7 copy-start.1

commit v7 on v6

--- a/solution.py
+++ b/solution.py
@@ -15,7 +15,7 @@
 
 def kernel(
     counts_any, cols_any, tv_hbm, p_hbm, out_ref,
-    counts, cols, tvb, a_own, a_in, a_mate, bb, give, keep, x2, zs, zr, cv, obuf,
+    counts, cols, tvb, a_own, a_in, a_mate, bb, give, keep, x2, zs, zr, cv,
     load_sem, a_send, a_recv, b_send, b_recv, e_send, e_recv, m_send, m_recv,
     x2_send, x2_recv, z_send, z_recv, c_send, c_recv, known,
 ):
@@ -212,13 +212,13 @@
 
         @pl.when(me)
         def _():
-            copy = pltpu.make_async_copy(cv.at[s], obuf.at[z], load_sem.at[0])
+            copy = pltpu.make_async_copy(cv.at[s], out_ref.at[pl.ds(z * PIECE, PIECE)], load_sem.at[0])
             copy.start()
             copy.wait()
 
         @pl.when(jnp.logical_not(me))
         def _():
-            remote(cv.at[s], obuf.at[z], c_send.at[s], c_recv, dev(j, owner_x, y, s0)).start()
+            remote(cv.at[s], out_ref.at[pl.ds(z * PIECE, PIECE)], c_send.at[s], c_recv, dev(j, owner_x, y, s0)).start()
 
     load_own.wait()
     take(1)
@@ -249,14 +249,12 @@
 
     @pl.when(has_own)
     def _():
-        others = obuf.at[pl.ds(0, NZ - 1)]
+        others = out_ref.at[pl.ds(0, (NZ - 1) * PIECE)]
         pltpu.make_async_copy(others, others, c_recv).wait()
 
     @pl.when(jnp.logical_not(has_own))
     def _():
-        pltpu.make_async_copy(obuf, obuf, c_recv).wait()
-
-    out_ref[...] = obuf[...].reshape(2 * TILE, TILE)
+        pltpu.make_async_copy(out_ref, out_ref, c_recv).wait()
 
     for copy in sent:
         copy.wait_send()
@@ -297,7 +295,6 @@
             pltpu.VMEM((STEPS, NZ, PIECE, TILE), f32),
             pltpu.VMEM((STEPS, NZ - 1, PIECE, TILE), f32),
             pltpu.VMEM((STEPS, PIECE, TILE), bf16),
-            pltpu.VMEM((NZ, PIECE, TILE), bf16),
             dma((4,)), dma, dma,
             dma((STEPS, 2)), dma((STEPS, 2)), dma((2, 2)), dma((2, 2)), dma((3,)), dma((3,)),
             dma((STEPS, 2)), dma((STEPS, 2)), dma((STEPS,)), dma((STEPS,)), dma((STEPS,)), dma,

time: 87.9 us -> 87.9 us (level)
  no operation moved by 1% of the time
where the time goes in v7:
time: 87.9 us; the launch traced here: 87.7 us
  Pallas kernels  86.4 us (98%)
  local copies, waits for them, and re-layouts  1.3 us (1%)
    pallas_call x1, Pallas kernels, per_device(): pl.pallas_call(kernel, out_shape=jax.ShapeDtypeStruct((2 * TILE, TILE), b...  86.4 us

profile of v7, /device:TPU:35, one launch (start us, length us, event | category | flops | bytes accessed | tf_op | source)
XLA Modules:
  0.0 87.7 jit_solution(2796577993090539909)
XLA Ops:
  0.0 0.0 copy-start
  0.0 0.0 copy-start.1
  0.0 0.7 copy-done
  0.7 0.0 copy-done.1
  0.7 86.4 %shard_map.46 = bf16[256,128]{1,0:T(8,128)(2,1)S(1)} custom-call(s32[1,12]{1,0:T(1,128)S(1)} %bitcast.2, s32[1,24]{1,0:T(1,128)S(1)} %bitcast.3, bf16[24,128,128]{2,1,0:T(8,128)(2,1)} %tv_hbm.1, bf16[1536,256]{1,0:T(8,128)(2,1)} %p_hbm.1), custom_call_target="tpu_custom_call" | custom-call | tf_op jit(solution)/shard_map/pallas_call | solution.py:274
  87.1 0.6 copy.6
Async XLA Ops:
  0.0 0.7 copy-start
  0.0 0.7 copy-start.1
